TPU v7x, 32 devices: a whole 2x2x4 slice. The times are simulated.
32 devices in a mesh: dp: 8 (over z, y), tensor: 4 (over x, core).
Axes of the slice: x: 2, y: 2, z: 4, core: 2. Of those that a mesh axis runs over, the one named last changes fastest.
Arguments:
- cotangent: bfloat16 [2048, 8192], P(('dp', 'tensor')), may hold values from -1.1048543 to 1.1048543
- gate_pre: bfloat16 [2048, 14336], P('dp', 'tensor'), may hold values from -5 to 5
- up_pre: bfloat16 [2048, 14336], P('dp', 'tensor'), may hold values from -28 to 28
- row_state: float32 [8192], P('dp'), may hold values from 0.02 to 3
- column_state: float32 [14336], P('tensor'), may hold values from 0.05 to 2
Outputs:
- update: float32 [8192, 14336], P('dp', 'tensor')
- row_next: float32 [8192], P('dp')
- column_next: float32 [14336], P('tensor')
- row_scale: float32 [1], replicated
All inputs are finite; a program needn't handle non-finite values.
Results may differ from a plain program's by a relative error of at most 0.019.
Values may be sent and summed in bfloat16 or wider, within the bound.
A program may use at most 192 MiB of HBM per device.

v0:
```python
import jax
import jax.numpy as jnp
from jax import lax
from jax.sharding import PartitionSpec as P

D = 8192
FF = 14336
EPSILON = 1e-30
DECAY_RATE = 0.9


def shards(cotangent, gate_pre, up_pre, row_state, column_state):
    hidden = (jax.nn.silu(gate_pre.astype(jnp.float32)) * up_pre.astype(jnp.float32)).astype(
        jnp.bfloat16
    )
    data_count = lax.axis_size("dp")
    tensor_count = lax.axis_size("tensor")
    spread = lax.all_to_all(cotangent, "dp", split_axis=1, concat_axis=0, tiled=True)
    tokens_all = lax.all_gather(spread, "tensor", axis=0, tiled=True)
    rows_each = cotangent.shape[0]
    block_rows = hidden.shape[0]
    blocks = tokens_all.reshape(tensor_count, data_count, rows_each, tokens_all.shape[1])
    incoming = lax.all_gather(hidden, "dp", axis=0, tiled=True)
    groups = incoming.shape[0] // block_rows
    shaped = incoming.reshape(groups, tensor_count, rows_each, incoming.shape[1])
    partial_value = jnp.einsum("jntd,njtf->ndf", blocks, shaped, preferred_element_type=jnp.float32)
    rounded = lax.optimization_barrier(partial_value.astype(jnp.bfloat16))
    gradient = jnp.sum(rounded.astype(jnp.float32), axis=0)
    squares = gradient * gradient + EPSILON
    column_part = jnp.sum(squares, axis=0)
    row_total = lax.psum(jnp.sum(squares, axis=1), "tensor")
    row_next = DECAY_RATE * row_state + (1.0 - DECAY_RATE) * row_total / FF
    column_total = lax.psum(column_part, "dp")
    row_sum_all = lax.psum(jnp.sum(row_next), "dp")
    column_next = DECAY_RATE * column_state + (1.0 - DECAY_RATE) * column_total / D
    row_mean = row_sum_all / D
    second_moment = row_next[:, None] * column_next[None, :] / row_mean
    raw_update = gradient / jnp.sqrt(second_moment)
    square_total = lax.psum(jnp.sum(raw_update * raw_update), ("dp", "tensor"))
    norm_value = jnp.sqrt(square_total / (float(D) * float(FF)))
    update = raw_update / jnp.maximum(1.0, norm_value)
    return (update, row_next, column_next, jnp.reshape(row_mean, (1,)))


def solution(mesh):
    return jax.shard_map(
        shards,
        mesh=mesh,
        in_specs=(
            P(("dp", "tensor"), None),
            P("dp", "tensor"),
            P("dp", "tensor"),
            P("dp"),
            P("tensor"),
        ),
        out_specs=(P("dp", "tensor"), P("dp"), P("tensor"), P()),
        check_vma=False,
    )
```

profile of v0, /device:TPU:12, one launch (start us, length us, event | category | flops | bytes accessed | tf_op | source)
XLA Modules:
  0.0 465.1 jit_solution(13334387134886437163)
XLA Ops:
  7.2 0.0 all-gather.5.cloned.1.call-start
  7.2 1.3 copy.20
  8.5 29.7 %all_to_all.19 = bf16[64,8,1024]{2,0,1:T(8,128)(2,1)} all-to-all(bf16[64,8,1024]{2,0,1:T(8,128)(2,1)S(1)} %bitcast.19), channel_id=1, replica_groups=mesh['dp'=8,'tensor'=4] {'dp'}, dimensions={1} | all-to-all | bytes 2097152 | tf_op jit(solution)/shard_map/all_to_all | solution.py:18
  38.2 0.0 all-gather.5.cloned.1.call-update
  38.2 0.0 all-gather.3.cloned.1.call-start
  38.3 4.4 fusion.8
  42.7 0.0 all-gather.3.cloned.1.call-update
  42.7 30.8 %all-gather.5.cloned.1.call-done = bf16[2048,1024]{1,0:T(8,128)(2,1)} async-done(((bf16[512,1024]{1,0:T(8,128)(2,1)}), bf16[2048,1024]{1,0:T(8,128)(2,1)}) %all-gather.5.cloned.1.call-update) | async-done | bytes 4194320 | tf_op jit(solution)/shard_map/all_gather | solution.py:19
  73.5 201.7 %all-gather.3.cloned.1.call-done = bf16[2048,3584]{1,0:T(8,128)(2,1)} async-done(((bf16[256,3584]{1,0:T(8,128)(2,1)}), bf16[2048,3584]{1,0:T(8,128)(2,1)}) %all-gather.3.cloned.1.call-update) | async-done | bytes 14680080 | tf_op jit(solution)/shard_map/all_gather | solution.py:23
  275.2 28.0 %fusion = bf16[8,1024,3584]{1,2,0:T(8,128)(2,1)} fusion(bf16[8,4,64,3584]{3,2,1,0:T(8,128)(2,1)} %bitcast.21, bf16[4,8,64,1024]{3,2,1,0:T(8,128)(2,1)} %bitcast.22), kind=kOutput, calls=%fused_computation.2 | convolution fusion | flops 15061745664 | bytes 77594624 | tf_op jit(solution)/shard_map/jntd,njtf->ndf/dot_general | solution.py:26
  303.2 24.8 %convert_reduce_fusion = f32[1024,3584]{0,1:T(8,128)} fusion(bf16[8,1024,3584]{1,2,0:T(8,128)(2,1)} %fusion), kind=kLoop, calls=%fused_computation.1 | loop fusion | flops 55050240 | bytes 73400320 | tf_op jit(solution)/shard_map/reduce_sum | solution.py:28
  328.0 0.0 copy-start.3
  328.0 0.0 copy-start.2
  328.0 7.7 %fusion.1 = (f32[3584]{0:T(1024)S(1)}, f32[1024]{0:T(1024)S(1)}) fusion(f32[1024,3584]{0,1:T(8,128)} %convert_reduce_fusion), kind=kLoop, calls=%fused_computation.6 | loop fusion | flops 14675456 | bytes 14698496 | tf_op jit(solution)/shard_map/reduce_sum | solution.py:30
  335.7 5.9 %psum.28 = f32[1024]{0:T(1024)S(1)} all-reduce(f32[1024]{0:T(1024)S(1)} %get-tuple-element.9), channel_id=1, replica_groups=mesh['dp'=8,'tensor'=4] {'tensor'}, use_global_device_ids=true, to_apply=%region_2.3 | all-reduce | flops 1024 | bytes 8192 | tf_op jit(solution)/shard_map/psum | solution.py:31
  341.5 0.0 copy-done.3
  341.5 0.6 fusion.9
  342.1 0.0 copy-start.1
  342.1 32.3 %all-reduce = (f32[]{:T(128)}, f32[3584]{0:T(1024)S(1)}) all-reduce(f32[]{:T(128)} %get-tuple-element.12, f32[3584]{0:T(1024)S(1)} %get-tuple-element.8), channel_id=1, replica_groups=mesh['dp'=8,'tensor'=4] {'dp'}, use_global_device_ids=true, to_apply=%region_6.7 | all-reduce | flops 3585 | bytes 28680 | tf_op jit(solution)/shard_map/psum | solution.py:34
  375.1 0.0 copy-done.2
  375.1 0.0 copy-start
  375.1 9.4 %multiply_reduce_fusion = f32[]{:T(128)} fusion(f32[1024,3584]{0,1:T(8,128)} %convert_reduce_fusion, f32[]{:T(128)} %div.42, f32[3584]{0:T(1024)S(1)} %multiply_add_fusion.1, f32[1024]{0:T(1024)S(1)} %get-tuple-element.13), kind=kLoop, calls=%fused_computation.3 | loop fusion | flops 18350080 | bytes 14698504 | tf_op jit(solution)/shard_map/reduce_sum | solution.py:39
  384.5 46.3 %psum.31 = f32[]{:T(128)} all-reduce(f32[]{:T(128)} %multiply_reduce_fusion), channel_id=1, replica_groups=mesh['dp'=8,'tensor'=4] {'dp','tensor'}, use_global_device_ids=true, to_apply=%region_8.9 | all-reduce | flops 1 | bytes 8 | tf_op jit(solution)/shard_map/psum | solution.py:39
  431.6 11.3 %broadcast_divide_fusion = f32[1024,3584]{0,1:T(8,128)} fusion(f32[]{:T(128)S(6)} %max_shard_map.3, f32[1024,3584]{0,1:T(8,128)} %convert_reduce_fusion, f32[]{:T(128)} %div.42, f32[3584]{0:T(1024)S(1)} %multiply_add_fusion.1, f32[1024]{0:T(1024)S(1)} %get-tuple-element.13), kind=kLoop, calls=%fused_computation.8 | loop fusion | flops 14680064 | bytes 29378568 | tf_op jit(solution)/shard_map/div | solution.py:41
  442.9 0.0 copy-done.1
  442.9 0.0 copy-done
  442.9 14.3 %copy.14 = f32[1024,3584]{1,0:T(8,128)} copy(f32[1024,3584]{0,1:T(8,128)} %broadcast_divide_fusion) | data formatting | bytes 29360128
  (1 shorter events, 0.0 us)
Async XLA Ops:
  7.2 66.4 %all-gather.5.cloned.1.call-start = ((), (), s32[]{:S(2)}) async-start(), calls=%async_computation.2 | async-start | bytes 5242880 | tf_op jit(solution)/shard_map/all_gather | solution.py:19
  38.2 237.0 %all-gather.3.cloned.1.call-start = ((), (), s32[]{:S(2)}) async-start(), calls=%async_computation.1 | async-start | bytes 16515072 | tf_op jit(solution)/shard_map/all_gather | solution.py:23
  328.0 13.5 %copy-start.3 = (f32[1024]{0:T(1024)S(1)}, f32[1024]{0:T(1024)}, u32[]{:S(2)}) copy-start(f32[1024]{0:T(1024)} %param.8) | copy-start | bytes 12292
  328.0 47.1 %copy-start.2 = (f32[3584]{0:T(1024)S(1)}, f32[3584]{0:T(1024)}, u32[]{:S(2)}) copy-start(f32[3584]{0:T(1024)} %param.9) | copy-start | bytes 43012
  342.1 100.7 %copy-start.1 = (f32[1024]{0:T(1024)}, f32[1024]{0:T(1024)S(1)}, u32[]{:S(2)}) copy-start(f32[1024]{0:T(1024)S(1)} %get-tuple-element.13) | copy-start | bytes 12292
  375.1 67.8 %copy-start = (f32[3584]{0:T(1024)}, f32[3584]{0:T(1024)S(1)}, u32[]{:S(2)}) copy-start(f32[3584]{0:T(1024)S(1)} %multiply_add_fusion.1) | copy-start | bytes 43012
Sparse Core Ops, SparseCore 0:
  38.4 35.1 all-gather.4
  76.3 198.8 all-gather.2
where the time goes:
time: 466 us; the launch traced here: 465 us
  waiting for transfers between devices  233 us (50%)
  blocking collectives  114 us (24%)
  other arithmetic  58.1 us (12%)
  matrix products  28 us (6%)
  between operations  16.6 us (4%)
  local copies, waits for them, and re-layouts  15.6 us (3%)
    all_gather x1, waiting for transfers between devices, shards(): incoming = lax.all_gather(hidden, 'dp', axis=0, tiled=True)  202 us
    psum x1, blocking collectives, shards(): square_total = lax.psum(jnp.sum(raw_update * raw_update), ('dp', 'tensor'))  46.3 us
    psum x1, blocking collectives, shards(): row_sum_all = lax.psum(jnp.sum(row_next), 'dp')  32.3 us
    all_gather x1, waiting for transfers between devices, shards(): tokens_all = lax.all_gather(spread, 'tensor', axis=0, tiled=True)  30.8 us
    all_to_all x1, blocking collectives, shards(): lax.all_to_all(cotangent, 'dp', split_axis=1, concat_axis=0, tiled=True)  29.7 us
    dot_general x1, matrix products, shards(): jnp.einsum('jntd,njtf->ndf', blocks, shaped, preferred_element_type=jnp.f...  28 us
    reduce_sum x1, other arithmetic, shards(): gradient = jnp.sum(rounded.astype(jnp.float32), axis=0)  24.8 us
    unnamed x9, local copies, waits for them, and re-layouts  14.3 us
  transfers between devices with their start and end apart: 2, of which 2 were waited for; matrix products, arithmetic and copies ran while one was open for 1% of the time, Pallas kernels for 0%

commit v1 on v0

--- a/solution.py
+++ b/solution.py
@@ -16,7 +16,14 @@
     data_count = lax.axis_size("dp")
     tensor_count = lax.axis_size("tensor")
     spread = lax.all_to_all(cotangent, "dp", split_axis=1, concat_axis=0, tiled=True)
-    tokens_all = lax.all_gather(spread, "tensor", axis=0, tiled=True)
+    size = lax.axis_size("tensor")
+    right = [(i, (i + 1) % size) for i in range(size)]
+    pieces = [spread]
+    for far in range(1, size):
+        pieces = [lax.ppermute(pieces[0], "tensor", right), *pieces]
+    result = jnp.concatenate(pieces, axis=0)
+    shift = (lax.axis_index("tensor") + 1) * pieces[-1].shape[0]
+    tokens_all = jnp.roll(result, shift, axis=0)
     rows_each = cotangent.shape[0]
     block_rows = hidden.shape[0]
     blocks = tokens_all.reshape(tensor_count, data_count, rows_each, tokens_all.shape[1])

time: 466 us -> 407 us (0.87)
  waiting for transfers between devices: 233 us -> 155 us
  blocking collectives: 114 us -> 140 us
  local copies, waits for them, and re-layouts: 15.6 us -> 6.91 us
    all_gather x1, waiting for transfers between devices: 202 us -> 112 us  [shards(): incoming = lax.all_gather(hidden, 'dp', axis=0, tiled=True)]
    ppermute x0 -> x3, waiting for transfers between devices: none -> 42.8 us  [shards(): pieces = [lax.ppermute(pieces[0], 'tensor', right), *pieces]]
    all_gather x1 -> x0, waiting for transfers between devices: 30.8 us -> none  [shards(): tokens_all = lax.all_gather(spread, 'tensor', axis=0, tiled=True)]
    all_to_all x1, blocking collectives: 29.7 us -> 55.4 us  [shards(): lax.all_to_all(cotangent, 'dp', split_axis=1, concat_axis=0, tiled=True)]
    unnamed x9 -> x15, local copies, waits for them, and re-layouts: 14.3 us -> 3.06 us
  transfers between devices with their start and end apart: 2 -> 4, of which waited for: 2 -> 4; matrix products, arithmetic and copies ran while one was open for 1% -> 2% of each run, Pallas kernels for 0% -> 0%
where the time goes in v1:
time: 407 us
  waiting for transfers between devices  155 us (38%)
  blocking collectives  140 us (34%)
  other arithmetic  60.3 us (15%)
  matrix products  27.8 us (7%)
  between operations  16.6 us (4%)
  local copies, waits for them, and re-layouts  6.91 us (2%)
    all_gather x1, waiting for transfers between devices, shards(): incoming = lax.all_gather(hidden, 'dp', axis=0, tiled=True)  112 us
    all_to_all x1, blocking collectives, shards(): lax.all_to_all(cotangent, 'dp', split_axis=1, concat_axis=0, tiled=True)  55.4 us
    psum x1, blocking collectives, shards(): square_total = lax.psum(jnp.sum(raw_update * raw_update), ('dp', 'tensor'))  46.3 us
    ppermute x3, waiting for transfers between devices, shards(): pieces = [lax.ppermute(pieces[0], 'tensor', right), *pieces]  42.8 us
    psum x1, blocking collectives, shards(): row_sum_all = lax.psum(jnp.sum(row_next), 'dp')  32.3 us
    dot_general x1, matrix products, shards(): jnp.einsum('jntd,njtf->ndf', blocks, shaped, preferred_element_type=jnp.f...  27.8 us
    reduce_sum x1, other arithmetic, shards(): gradient = jnp.sum(rounded.astype(jnp.float32), axis=0)  25.2 us
    div x1, other arithmetic, shards(): update = raw_update / jnp.maximum(1.0, norm_value)  11.2 us
  transfers between devices with their start and end apart: 4, of which 4 were waited for; matrix products, arithmetic and copies ran while one was open for 2% of the time, Pallas kernels for 0%

profile of v1, /device:TPU:12, one launch (start us, length us, event | category | flops | bytes accessed | tf_op | source)
XLA Modules:
  0.0 406.8 jit_solution(7014774828081869802)
XLA Ops:
  7.2 0.0 all-gather.2.cloned.1.call-start
  7.2 4.4 %fusion.7 = bf16[256,3584]{1,0:T(8,128)(2,1)} fusion(bf16[256,3584]{1,0:T(8,128)(2,1)} %param.7, bf16[256,3584]{1,0:T(8,128)(2,1)} %param.6), kind=kLoop, calls=%fused_computation.15 | loop fusion | flops 7340032 | bytes 5505024 | tf_op jit(solution)/shard_map/convert_element_type | solution.py:13
  11.6 0.0 all-gather.2.cloned.1.call-update
  11.6 1.3 copy.19
  13.0 55.4 %all_to_all.19 = bf16[64,8,1024]{2,0,1:T(8,128)(2,1)S(1)} all-to-all(bf16[64,8,1024]{2,0,1:T(8,128)(2,1)S(1)} %bitcast.17), channel_id=1, replica_groups=mesh['dp'=8,'tensor'=4] {'dp'}, dimensions={1} | all-to-all | bytes 2097152 | tf_op jit(solution)/shard_map/all_to_all | solution.py:18
  68.4 0.0 collective-permute-start
  68.4 14.2 %collective-permute-done = bf16[512,1024]{1,0:T(8,128)(2,1)S(1)} collective-permute-done((bf16[512,1024]{1,0:T(8,128)(2,1)S(1)}, bf16[512,1024]{1,0:T(8,128)(2,1)S(1)}, u32[]{:S(2)}, u32[]{:S(2)}) %collective-permute-start) | collective-permute-done | bytes 1048608 | tf_op jit(solution)/shard_map/ppermute | solution.py:23
  82.6 0.0 collective-permute-start.1
  82.6 14.2 %collective-permute-done.1 = bf16[512,1024]{1,0:T(8,128)(2,1)S(1)} collective-permute-done((bf16[512,1024]{1,0:T(8,128)(2,1)S(1)}, bf16[512,1024]{1,0:T(8,128)(2,1)S(1)}, u32[]{:S(2)}, u32[]{:S(2)}) %collective-permute-start.1) | collective-permute-done | bytes 1048608 | tf_op jit(solution)/shard_map/ppermute | solution.py:23
  96.8 0.0 collective-permute-start.2
  96.8 14.3 %collective-permute-done.2 = bf16[512,1024]{1,0:T(8,128)(2,1)} collective-permute-done((bf16[512,1024]{1,0:T(8,128)(2,1)S(1)}, bf16[512,1024]{1,0:T(8,128)(2,1)}, u32[]{:S(2)}, u32[]{:S(2)}) %collective-permute-start.2) | collective-permute-done | bytes 1048608 | tf_op jit(solution)/shard_map/ppermute | solution.py:23
  111.2 1.4 constant_dynamic-update-slice_fusion.7
  112.6 0.1 constant_dynamic-update-slice_fusion.6
  112.6 0.1 constant_dynamic-update-slice_fusion.5
  112.7 0.1 constant_dynamic-update-slice_fusion.4
  112.8 1.3 constant_dynamic-update-slice_fusion.3
  114.1 0.1 constant_dynamic-update-slice_fusion.2
  114.2 0.1 constant_dynamic-update-slice_fusion.1
  114.3 0.1 constant_dynamic-update-slice_fusion
  114.3 2.5 constant_dynamic-slice_fusion
  116.8 112.4 %all-gather.2.cloned.1.call-done = bf16[2048,3584]{1,0:T(8,128)(2,1)} async-done(((bf16[256,3584]{1,0:T(8,128)(2,1)}), bf16[2048,3584]{1,0:T(8,128)(2,1)}) %all-gather.2.cloned.1.call-update) | async-done | bytes 14680080 | tf_op jit(solution)/shard_map/all_gather | solution.py:30
  229.2 27.8 %bitcast_convert_fusion = bf16[8,1024,3584]{2,1,0:T(8,128)(2,1)} fusion(bf16[4,8,64,1024]{3,2,1,0:T(8,128)(2,1)} %bitcast.16, bf16[8,4,64,3584]{3,2,1,0:T(8,128)(2,1)} %bitcast.19), kind=kOutput, calls=%fused_computation | convolution fusion | flops 15061745664 | bytes 77594624 | tf_op jit(solution)/shard_map/jntd,njtf->ndf/dot_general | solution.py:33
  257.0 25.2 %convert_reduce_fusion = f32[1024,3584]{1,0:T(8,128)} fusion(bf16[8,1024,3584]{2,1,0:T(8,128)(2,1)} %bitcast_convert_fusion), kind=kLoop, calls=%fused_computation.1 | loop fusion | flops 55050240 | bytes 73400320 | tf_op jit(solution)/shard_map/reduce_sum | solution.py:35
  282.2 0.0 copy-start.3
  282.2 0.0 copy-start.2
  282.2 10.6 %fusion.1 = (f32[3584]{0:T(1024)S(1)}, f32[1024]{0:T(1024)S(1)}) fusion(f32[1024,3584]{1,0:T(8,128)} %convert_reduce_fusion), kind=kLoop, calls=%fused_computation.6 | loop fusion | flops 14675456 | bytes 14698496 | tf_op jit(solution)/shard_map/reduce_sum | solution.py:37
  292.9 5.9 %psum.28 = f32[1024]{0:T(1024)S(1)} all-reduce(f32[1024]{0:T(1024)S(1)} %get-tuple-element.5), channel_id=1, replica_groups=mesh['dp'=8,'tensor'=4] {'tensor'}, use_global_device_ids=true, to_apply=%region_2.3 | all-reduce | flops 1024 | bytes 8192 | tf_op jit(solution)/shard_map/psum | solution.py:38
  298.7 0.0 copy-done.3
  298.7 0.6 fusion.8
  299.3 0.0 copy-start.1
  299.3 32.3 %all-reduce = (f32[]{:T(128)}, f32[3584]{0:T(1024)S(1)}) all-reduce(f32[]{:T(128)} %get-tuple-element.8, f32[3584]{0:T(1024)S(1)} %get-tuple-element.4), channel_id=1, replica_groups=mesh['dp'=8,'tensor'=4] {'dp'}, use_global_device_ids=true, to_apply=%region_6.7 | all-reduce | flops 3585 | bytes 28680 | tf_op jit(solution)/shard_map/psum | solution.py:41
  332.3 0.0 copy-done.2
  332.3 0.0 copy-start
  332.3 8.3 %multiply_reduce_fusion = f32[]{:T(128)} fusion(f32[1024,3584]{1,0:T(8,128)} %convert_reduce_fusion, f32[]{:T(128)} %div.42, f32[3584]{0:T(1024)S(1)} %multiply_add_fusion.1, f32[1024]{0:T(1024)S(1)} %get-tuple-element.9), kind=kLoop, calls=%fused_computation.3 | loop fusion | flops 18350080 | bytes 14698504 | tf_op jit(solution)/shard_map/reduce_sum | solution.py:46
  340.6 46.3 %psum.31 = f32[]{:T(128)} all-reduce(f32[]{:T(128)} %multiply_reduce_fusion), channel_id=1, replica_groups=mesh['dp'=8,'tensor'=4] {'dp','tensor'}, use_global_device_ids=true, to_apply=%region_8.9 | all-reduce | flops 1 | bytes 8 | tf_op jit(solution)/shard_map/psum | solution.py:46
  387.7 11.2 %broadcast_divide_fusion = f32[1024,3584]{1,0:T(8,128)} fusion(f32[]{:T(128)S(6)} %max_shard_map.3, f32[1024,3584]{1,0:T(8,128)} %convert_reduce_fusion, f32[]{:T(128)} %div.42, f32[3584]{0:T(1024)S(1)} %multiply_add_fusion.1, f32[1024]{0:T(1024)S(1)} %get-tuple-element.9), kind=kLoop, calls=%fused_computation.8 | loop fusion | flops 14680064 | bytes 29378568 | tf_op jit(solution)/shard_map/div | solution.py:48
  398.9 0.0 copy-done.1
  398.9 0.0 copy-done
  (1 shorter events, 0.0 us)
Async XLA Ops:
  7.2 222.1 %all-gather.2.cloned.1.call-start = ((), (), s32[]{:S(2)}) async-start(), calls=%async_computation.1 | async-start | bytes 16515072 | tf_op jit(solution)/shard_map/all_gather | solution.py:30
  68.4 14.2 %collective-permute-start = (bf16[512,1024]{1,0:T(8,128)(2,1)S(1)}, bf16[512,1024]{1,0:T(8,128)(2,1)S(1)}, u32[]{:S(2)}, u32[]{:S(2)}) collective-permute-start(bf16[512,1024]{1,0:T(8,128)(2,1)S(1)} %bitcast.13), channel_id=1, source_target_pairs={{0,1},{1,2},{2,3},{3,0},{4,5},{5,6},{6,7},{7,4},{8,9},{9,10},{10,1... | collective-permute-start | bytes 3145736 | tf_op jit(solution)/shard_map/ppermute | solution.py:23
  82.6 14.2 %collective-permute-start.1 = (bf16[512,1024]{1,0:T(8,128)(2,1)S(1)}, bf16[512,1024]{1,0:T(8,128)(2,1)S(1)}, u32[]{:S(2)}, u32[]{:S(2)}) collective-permute-start(bf16[512,1024]{1,0:T(8,128)(2,1)S(1)} %collective-permute-done), channel_id=1, source_target_pairs={{0,1},{1,2},{2,3},{3,0},{4,5},{5,6},{6,7},{7,4},{8,9},{9,10},{10,1... | collective-permute-start | bytes 3145736 | tf_op jit(solution)/shard_map/ppermute | solution.py:23
  96.8 14.3 %collective-permute-start.2 = (bf16[512,1024]{1,0:T(8,128)(2,1)S(1)}, bf16[512,1024]{1,0:T(8,128)(2,1)}, u32[]{:S(2)}, u32[]{:S(2)}) collective-permute-start(bf16[512,1024]{1,0:T(8,128)(2,1)S(1)} %collective-permute-done.1), channel_id=1, source_target_pairs={{0,1},{1,2},{2,3},{3,0},{4,5},{5,6},{6,7},{7,4},{8,9},{9,10},{10,1... | collective-permute-start | bytes 3145736 | tf_op jit(solution)/shard_map/ppermute | solution.py:23
  282.2 16.5 %copy-start.3 = (f32[1024]{0:T(1024)S(1)}, f32[1024]{0:T(1024)}, u32[]{:S(2)}) copy-start(f32[1024]{0:T(1024)} %param.8) | copy-start | bytes 12292
  282.2 50.0 %copy-start.2 = (f32[3584]{0:T(1024)S(1)}, f32[3584]{0:T(1024)}, u32[]{:S(2)}) copy-start(f32[3584]{0:T(1024)} %param.9) | copy-start | bytes 43012
  299.3 99.5 %copy-start.1 = (f32[1024]{0:T(1024)}, f32[1024]{0:T(1024)S(1)}, u32[]{:S(2)}) copy-start(f32[1024]{0:T(1024)S(1)} %get-tuple-element.9) | copy-start | bytes 12292
  332.3 66.6 %copy-start = (f32[3584]{0:T(1024)}, f32[3584]{0:T(1024)S(1)}, u32[]{:S(2)}) copy-start(f32[3584]{0:T(1024)S(1)} %multiply_add_fusion.1) | copy-start | bytes 43012
Sparse Core Ops, SparseCore 0:
  11.8 217.4 all-gather.1
